TPU v7x, 32 devices: a whole 2x2x4 slice. The times are simulated.
32 devices in a mesh: seq: 8 (over z, x), mp: 4 (over y, core).
Axes of the slice: x: 2, y: 2, z: 4, core: 2. Of those that a mesh axis runs over, the one named last changes fastest.
Arguments:
- tokens: bfloat16 [2048, 2560], P('seq'), may hold values from -6 to 6
- w_in: bfloat16 [2560, 4096], P('seq', 'mp'), may hold values from -0.125 to 0.125
- b_in: float32 [2048, 128], P('seq'), may hold values from -0.6 to 0.6
- c_in: float32 [2048, 128], P('seq'), may hold values from -0.6 to 0.6
- dt: float32 [64, 2048], P('mp', 'seq'), may hold values from 0.05 to 0.2
- log_rate: float32 [64], P('mp'), as said below
- cot: bfloat16 [2048, 4096], P('seq', 'mp'), may hold values from -6 to 6
Outputs:
- mixed: bfloat16 [2048, 4096], P('seq', 'mp')
- direction: float32 [2560, 4096], P('seq', 'mp')
- perturbed: float32 [2560, 4096], P('seq', 'mp')
- perturbed_rate: float32 [64], P('mp')
Inputs may be any that keep to these rules, and one draw needn't show every extreme that they name: exp(log_rate) lies between 1 / 2048 and 0.5; some heads decay within some tens of tokens, others keep their state over the whole sequence.
All inputs are finite; a program needn't handle non-finite values.
Results may differ from a plain program's by a relative error of at most 0.0049.
Values may be sent and summed in bfloat16 or wider, within the bound.
A program may use at most 128 MiB of HBM per device.

v0:
```python
import math

import jax
import jax.numpy as jnp
from jax import lax
from jax.sharding import PartitionSpec as P

D = 2560
H = 64
P_SIZE = 64
N = 128
Q = 256


HIGH = lax.Precision.HIGHEST
ascent = 0.05
rate_ascent = 0.5


def entering(part, axis, combine, identity, reverse):
    count = lax.axis_size(axis)
    place = lax.axis_index(axis)
    ahead = count - 1 - place if reverse else place
    gathered = jax.tree.map(lambda a: lax.all_gather(a, axis), part)
    state = jax.tree.map(lambda a, e: jnp.zeros_like(a) + jnp.asarray(e, a.dtype), part, identity)

    def one(step, state):
        source = count - 1 - step if reverse else step
        return combine(
            state, jax.tree.map(lambda a: lax.dynamic_index_in_dim(a, source, 0, False), gathered)
        )

    return lax.fori_loop(0, ahead, one, state)


def span_core(b_blk, c_blk, logdec):
    width = logdec.shape[1]
    cum = jnp.cumsum(logdec, axis=1)
    places = jnp.arange(width)
    lower = (places[:, None] >= places[None, :])[None]
    gap = cum[:, :, None] - cum[:, None, :]
    blend = jnp.where(lower, jnp.exp(jnp.where(lower, gap, 0.0)), 0.0)
    scores = jnp.dot(c_blk, b_blk.T, precision=HIGH)
    return (cum, gap, blend * scores[None])


def span_forward(x_blk, dt_blk, b_blk, cum, kern):
    kern_x = kern * dt_blk[:, None, :]
    y_local = jnp.einsum("hts,shp->thp", kern_x, x_blk, precision=HIGH)
    final = cum[:, -1]
    tail = (jnp.exp(final[:, None] - cum) * dt_blk).T
    state = jnp.einsum("sn,shp->hnp", b_blk, x_blk * tail[:, :, None], precision=HIGH)
    return (y_local, jnp.exp(final), state)


def span_entry(c_blk, cum, h_in):
    return jnp.einsum("tn,hnp->thp", c_blk, h_in, precision=HIGH) * jnp.exp(cum).T[:, :, None]


def span_lead(c_blk, cot_blk, cum):
    return jnp.einsum("tn,thp->hnp", c_blk, cot_blk * jnp.exp(cum).T[:, :, None], precision=HIGH)


def span_backward(x_blk, cot_blk, dt_blk, b_blk, cum, gap, kern, entry, h_in, after):
    final = cum[:, -1]
    kern_x = kern * dt_blk[:, None, :]
    back = jnp.einsum("hts,thp->shp", kern, cot_blk, precision=HIGH)
    fall = jnp.exp(final[:, None] - cum).T
    proj = jnp.einsum("sn,hnp->shp", b_blk, after, precision=HIGH)
    grad_x = dt_blk.T[:, :, None] * (back + fall[:, :, None] * proj)
    pairs = jnp.einsum("thp,shp->hts", cot_blk, x_blk, precision=HIGH)
    part = jnp.sum(kern_x * gap * pairs, axis=(1, 2))
    part = part + jnp.sum(jnp.sum(entry * cot_blk, axis=2) * cum.T, axis=0)
    weight = fall * dt_blk.T * (final[:, None] - cum).T
    part = part + jnp.sum(weight * jnp.sum(proj * x_blk, axis=2), axis=0)
    part = part + jnp.exp(final) * final * jnp.sum(after * h_in, axis=(1, 2))
    return (grad_x, part)


def compose(earlier, later):
    return (earlier[0] * later[0], later[0][:, None, None] * earlier[1] + later[1])


def body(tokens, w_in, b_in, c_in, dt, log_rate, cot):
    rows = tokens.shape[0]
    width_loc = w_in.shape[1]
    heads = width_loc // P_SIZE
    blocks = rows // Q
    columns = tokens
    x_bf = jnp.dot(
        columns, lax.all_gather(w_in, "seq", axis=0, tiled=True), preferred_element_type=jnp.float32
    ).astype(jnp.bfloat16)
    x_all = x_bf.astype(jnp.float32).reshape(rows, heads, P_SIZE)
    cot_all = cot.astype(jnp.float32).reshape(rows, heads, P_SIZE)
    logdec = -dt * jnp.exp(log_rate)[:, None]
    ones = jnp.ones((heads,), jnp.float32)
    zero_state = jnp.zeros((heads, N, P_SIZE), jnp.float32)
    fwd_pair = (ones, zero_state)
    block = 0
    x_blk = x_all
    cot_blk = cot_all
    dt_blk = dt
    b_blk = b_in
    c_blk = c_in
    cum, gap, kern = span_core(b_blk, c_blk, logdec)
    y_local, decay, state = span_forward(x_blk, dt_blk, b_blk, cum, kern)
    lead = span_lead(c_blk, cot_blk, cum)
    saved = [(x_blk, cot_blk, dt_blk, b_blk, c_blk, cum, gap, kern, y_local, decay, state, lead)]
    fwd_pair = compose(fwd_pair, (decay, state))
    bwd_pair = (ones, zero_state)
    for block in reversed(range(blocks)):
        bwd_pair = compose(bwd_pair, (saved[block][9], saved[block][11]))
    prior = entering(fwd_pair, "seq", compose, (ones, zero_state), False)[1]
    later = entering(bwd_pair, "seq", compose, (ones, zero_state), True)[1]
    block = 0
    x_blk, cot_blk, dt_blk, b_blk, c_blk, cum, gap, kern, y_local, decay, state, lead = saved[block]
    entry = span_entry(c_blk, cum, prior)
    y_blocks = y_local + entry
    entries = [entry]
    h_ins = [prior]
    mixed = y_blocks.reshape(rows, width_loc).astype(jnp.bfloat16)
    gx_blocks = [None] * blocks
    rate_part = jnp.zeros((heads - 0,), jnp.float32)
    after = later
    for block in reversed(range(blocks)):
        x_blk, cot_blk, dt_blk, b_blk, c_blk, cum, gap, kern, y_local, decay, state, lead = saved[
            block
        ]
        grad_x, part = span_backward(
            x_blk, cot_blk, dt_blk, b_blk, cum, gap, kern, entries[block], h_ins[block], after
        )
        gx_blocks[block] = grad_x
        rate_part = rate_part + part
        after = decay[0:heads, None, None] * after + lead
    gx_part = gx_blocks[0].reshape(rows, (heads - 0) * P_SIZE).astype(jnp.bfloat16)
    gx_bf, rate_part = (gx_part, rate_part)
    columns = tokens
    grad_w = lax.psum_scatter(
        lax.dot_general(
            columns, gx_bf, (((0,), (0,)), ((), ())), preferred_element_type=jnp.float32
        ),
        "seq",
        scatter_dimension=0,
        tiled=True,
    )
    squares = jnp.sum(grad_w * grad_w)
    grad_rate, seq_squares = lax.psum((rate_part, squares), "seq")
    rate_local = jnp.sum(grad_rate * grad_rate)
    total, rate_sq = lax.psum((seq_squares + rate_local, rate_local), "mp")
    scale = 1.0 / jnp.maximum(jnp.sqrt(total), 1.0)
    rate_scale = math.sqrt(H) / jnp.maximum(jnp.sqrt(rate_sq), 1.0)
    direction = grad_w * (math.sqrt(D * H * P_SIZE) * scale)
    perturbed = w_in.astype(jnp.float32) + ascent * scale * grad_w
    perturbed_rate = log_rate + rate_ascent * rate_scale * grad_rate
    return (mixed, direction, perturbed, perturbed_rate)


def solution(mesh):
    in_specs = (
        P("seq", None),
        P("seq", "mp"),
        P("seq", None),
        P("seq", None),
        P("mp", "seq"),
        P("mp"),
        P("seq", "mp"),
    )
    out_specs = (P("seq", "mp"), P("seq", "mp"), P("seq", "mp"), P("mp"))
    return jax.shard_map(body, mesh=mesh, in_specs=in_specs, out_specs=out_specs, check_vma=False)
```

profile of v0, /device:TPU:0, one launch (start us, length us, event | category | flops | bytes accessed | tf_op | source)
XLA Modules:
  0.0 482.8 jit_solution(3878543051226144569)
XLA Ops:
  13.6 2.7 fusion.44
  16.5 82.3 %all-gather.7.cloned.1.call-done = bf16[2560,1024]{1,0:T(8,128)(2,1)} async-done(((bf16[320,1024]{1,0:T(8,128)(2,1)}), bf16[2560,1024]{1,0:T(8,128)(2,1)}) %all-gather.7.cloned.1.call-update) | async-done | bytes 5242896 | tf_op jit(solution)/shard_map/all_gather | solution.py:91
  98.8 4.0 convolution_convert_fusion
  103.0 1.8 fusion.43
  106.4 19.4 %all-reduce = f32[128]{0:T(128)S(1)} all-reduce(f32[128]{0:T(128)S(1)} %dynamic-update-slice), channel_id=2, replica_groups=mesh['seq'=8,'mp'=4] {'seq'}, use_global_device_ids=true, to_apply=%add | all-reduce | flops 128 | bytes 1024
  128.3 44.5 %all-gather.11.cloned.1.call-done = f32[128,128,64]{1,2,0:T(8,128)} async-done(((f32[16,128,64]{1,2,0:T(8,128)}), f32[128,128,64]{1,2,0:T(8,128)}) %all-gather.11.cloned.1.call-update) | async-done | bytes 4194320 | tf_op jit(solution)/shard_map/all_gather | solution.py:24
  172.9 38.5 %while.27 = (s32[]{:T(128)}, f32[16,128,64]{2,1,0:T(8,128)S(1)}, s32[]{:T(128)}, f32[8,16]{1,0:T(8,128)}, f32[8,16,128,64]{2,3,1,0:T(8,128)}, /*index=5*/s32[]{:T(128)}, s32[]{:T(128)}, s32[]{:T(128)}, s32[]{:T(128)}) while((s32[]{:T(128)}, f32[16,128,64]{2,1,0:T(8,128)S(1)}, s32[]{:T(128)}, f32[8,16]{1,0:T(8,128)}, ...), condition=%wide.region_5.6_spmd, body=%wide.region_4.5_spmd.sunk | while | flops 262150 | bytes 3670363 | solution.py:33
  174.2 1.9 constant_dynamic-slice_fusion.5
  179.7 1.9 constant_dynamic-slice_fusion.5
  181.6 1.4 copy.83
  185.2 1.9 constant_dynamic-slice_fusion.5
  190.7 1.9 constant_dynamic-slice_fusion.5
  196.2 1.9 constant_dynamic-slice_fusion.5
  201.7 1.9 constant_dynamic-slice_fusion.5
  207.1 2.0 constant_dynamic-slice_fusion.5
  211.5 3.9 fusion.45
  215.4 5.0 %fusion.40 = bf16[256,16,64]{0,2,1:T(8,128)(2,1)S(1)} fusion(bf16[256,16,64]{0,2,1:T(8,128)(2,1)} %bitcast.128, f32[256,256]{0,1:T(8,128)} %fusion.60, f32[16,256]{1,0:T(8,128)} %copy-done.16, pred[256,256]{0,1:T(8,128)(4,1)} %iota_compare_fusion, f32[256,16,64]{0,2,1:T(8,128)S(1)} %get-tuple-element.212, f32[256,16]{0,1:T(8,128)} %get-tuple-element.206, ...), kind=kOutput, calls=%fused_computation.44 | convolution fusion | flops 810549248 | bytes 2473984 | tf_op jit(solution)/shard_map/hts,thp->shp/dot_general | solution.py:67
  220.5 5.4 %convolution_bitcast_fusion = f32[2560,1024]{0,1:T(8,128)} fusion(bf16[256,1024]{0,1:T(8,128)(2,1)S(1)} %bitcast.132, bf16[256,2560]{1,0:T(8,128)(2,1)S(1)} %copy-done), kind=kOutput, calls=%fused_computation.6 | convolution fusion | flops 1342177280 | bytes 12320768 | tf_op jit(solution)/shard_map/dot_general | solution.py:139
  225.8 11.4 %copy.62 = f32[2560,1024]{1,0:T(8,128)} copy(f32[2560,1024]{0,1:T(8,128)} %convolution_bitcast_fusion) | data formatting | bytes 20971520
  239.5 3.2 fusion.9
  242.7 4.1 all-gather.9.cloned.1.call-done
  247.2 3.9 fusion.46
  252.1 1.5 multiply_reduce_fusion.1
  253.6 173.5 %reduce-scatter.4.cloned.1.call-done = f32[320,1024]{1,0:T(8,128)} async-done(((f32[2560,1024]{1,0:T(8,128)}), f32[320,1024]{1,0:T(8,128)}) %reduce-scatter.4.cloned.1.call-update) | async-done | bytes 1310736
  427.1 1.8 copy.63
  429.9 5.3 %fusion.37 = bf16[256,16,64]{0,2,1:T(8,128)(2,1)} fusion(f32[256,16,64]{0,2,1:T(8,128)} %get-tuple-element.210, bf16[256,16,64]{0,2,1:T(8,128)(2,1)S(1)} %bitcast.126, f32[16,256]{1,0:T(8,128)S(1)} %copy-done.13, f32[256,256]{0,1:T(8,128)} %fusion.60, f32[16,256]{1,0:T(8,128)S(1)} %copy-done.18, pred[256,256]{0,1:T(8,128)(4,1)S(1)} %copy-done.15), kind=kOutput, calls=%fused_computation.42 | convolution fusion | flops 811073536 | bytes 2457600 | tf_op jit(solution)/shard_map/hts,shp->thp/dot_general | solution.py:49
  435.3 20.0 %all-reduce.1 = (f32[]{:T(128)}, f32[16]{0:T(128)S(1)}) all-reduce(f32[]{:T(128)} %multiply_reduce_fusion, f32[16]{0:T(128)S(1)} %fusion.57), channel_id=1, replica_groups=mesh['seq'=8,'mp'=4] {'seq'}, use_global_device_ids=true, to_apply=%region_8.9 | all-reduce | flops 17 | bytes 136 | tf_op jit(solution)/shard_map/psum | solution.py:147
  457.2 2.0 copy.54
  459.2 6.3 %all-reduce.2 = (f32[]{:T(128)}, f32[]{:T(128)}) all-reduce(f32[]{:T(128)S(6)} %add.94, f32[]{:T(128)} %multiply_reduce_fusion.2), channel_id=1, replica_groups=mesh['seq'=8,'mp'=4] {'mp'}, use_global_device_ids=true, to_apply=%region_17.18 | all-reduce | flops 2 | bytes 16 | tf_op jit(solution)/shard_map/psum | solution.py:149
  467.5 3.0 multiply_add_fusion
  470.5 2.9 copy.56
  473.4 2.9 copy.55
  (105 shorter events, 39.3 us)
Async XLA Ops:
  7.2 91.6 %copy-start = (bf16[256,2560]{1,0:T(8,128)(2,1)S(1)}, bf16[256,2560]{1,0:T(8,128)(2,1)}, u32[]{:S(2)}) copy-start(bf16[256,2560]{1,0:T(8,128)(2,1)} %param.11) | copy-start | bytes 3932164
  7.2 91.6 %all-gather.7.cloned.1.call-start = ((), (), s32[]{:S(2)}) async-start(), calls=%async_computation.1 | async-start | bytes 5898240 | tf_op jit(solution)/shard_map/all_gather | solution.py:91
  7.9 164.9 %all-gather.11.cloned.1.call-start = ((), (), s32[]{:S(2)}) async-start(), calls=%async_computation.3 | async-start | bytes 4718592 | tf_op jit(solution)/shard_map/all_gather | solution.py:24
  10.2 6.1 %copy-start.19 = (f32[16,2]{0,1:T(2,128)}, f32[16,2]{0,1:T(2,128)S(1)}, u32[]{:S(2)}) copy-start(f32[16,2]{0,1:T(2,128)S(1)} %slice.11) | copy-start | bytes 388
  11.4 87.4 %copy-start.5 = (bf16[256,1024]{0,1:T(8,128)(2,1)}, bf16[256,1024]{0,1:T(8,128)(2,1)S(1)}, u32[]{:S(2)}) copy-start(bf16[256,1024]{0,1:T(8,128)(2,1)S(1)} %copy.49) | copy-start | bytes 1572868
  11.5 0.7 copy-start.16
  11.7 4.6 copy-start.20
  13.6 2.7 copy-start.11
  16.4 86.7 %copy-start.9 = (f32[256,128]{1,0:T(8,128)S(1)}, f32[256,128]{1,0:T(8,128)}, u32[]{:S(2)}) copy-start(f32[256,128]{1,0:T(8,128)} %param.13) | copy-start | bytes 393220
  16.4 88.5 %copy-start.24 = (u32[32]{0:T(128)S(1)}, u32[32]{0:T(128)}, u32[]{:S(2)}) copy-start(u32[32]{0:T(128)} %constant.76) | copy-start | bytes 388
  16.4 110.8 %copy-start.8 = (f32[256,128]{1,0:T(8,128)S(1)}, f32[256,128]{1,0:T(8,128)}, u32[]{:S(2)}) copy-start(f32[256,128]{1,0:T(8,128)} %param.14) | copy-start | bytes 393220
  16.4 230.5 %all-gather.9.cloned.1.call-start = ((), (), s32[]{:S(2)}) async-start(), calls=%async_computation.2 | async-start | bytes 4718592 | tf_op jit(solution)/shard_map/all_gather | solution.py:24
  103.0 69.8 %copy-start.2 = (bf16[256,1024]{0,1:T(8,128)(2,1)}, bf16[256,1024]{0,1:T(8,128)(2,1)S(1)}, u32[]{:S(2)}) copy-start(bf16[256,1024]{0,1:T(8,128)(2,1)S(1)} %copy.42) | copy-start | bytes 1572868
  104.9 322.2 %reduce-scatter.4.cloned.1.call-start = ((), (), s32[]{:S(2)}) async-start(), calls=%async_computation.4 | async-start | bytes 11796480
  211.5 9.0 %copy-start.1 = (f32[16,128,64]{2,1,0:T(8,128)}, f32[16,128,64]{2,1,0:T(8,128)S(1)}, u32[]{:S(2)}) copy-start(f32[16,128,64]{2,1,0:T(8,128)S(1)} %get-tuple-element.133) | copy-start | bytes 1572868
  237.2 1.1 copy-start.7
  237.2 2.3 copy-start.3
  237.2 2.3 copy-start.6
  237.2 2.3 copy-start.10
  237.2 2.2 copy-start.12
  237.3 2.2 copy-start.14
  237.3 2.2 copy-start.17
  247.2 6.4 %copy-start.21 = (f32[16]{0:T(128)S(1)}, f32[16]{0:T(128)}, u32[]{:S(2)}) copy-start(f32[16]{0:T(128)} %copy-done.20) | copy-start | bytes 196
  247.2 6.4 %copy-start.23 = (f32[16]{0:T(128)S(1)}, f32[16]{0:T(128)}, u32[]{:S(2)}) copy-start(f32[16]{0:T(128)} %fusion.9) | copy-start | bytes 196
  247.2 182.7 %copy-start.4 = (bf16[256,1024]{0,1:T(8,128)(2,1)S(1)}, bf16[256,1024]{0,1:T(8,128)(2,1)}, u32[]{:S(2)}) copy-start(bf16[256,1024]{0,1:T(8,128)(2,1)} %copy-done.2) | copy-start | bytes 1572868
  251.2 178.7 %copy-start.13 = (f32[16,256]{1,0:T(8,128)S(1)}, f32[16,256]{1,0:T(8,128)}, u32[]{:S(2)}) copy-start(f32[16,256]{1,0:T(8,128)} %param.15) | copy-start | bytes 49156
  251.2 178.7 %copy-start.15 = (pred[256,256]{0,1:T(8,128)(4,1)S(1)}, pred[256,256]{0,1:T(8,128)(4,1)}, u32[]{:S(2)}) copy-start(pred[256,256]{0,1:T(8,128)(4,1)} %iota_compare_fusion) | copy-start | bytes 196612
  251.2 178.7 %copy-start.18 = (f32[16,256]{1,0:T(8,128)S(1)}, f32[16,256]{1,0:T(8,128)}, u32[]{:S(2)}) copy-start(f32[16,256]{1,0:T(8,128)} %copy-done.16) | copy-start | bytes 49156
  429.9 37.1 %copy-start.22 = (f32[16]{0:T(128)S(1)}, f32[16]{0:T(128)}, u32[]{:S(2)}) copy-start(f32[16]{0:T(128)} %param.16) | copy-start | bytes 196
Sparse Core Ops, SparseCore 0:
  10.2 88.5 all-gather.6
  101.5 71.2 all-gather.10
  175.5 71.3 all-gather.8
  250.3 176.7 reduce-scatter.3
where the time goes:
time: 485 us; the launch traced here: 483 us
  waiting for transfers between devices  305 us (63%)
  local copies, waits for them, and re-layouts  60 us (12%)
  blocking collectives  45.7 us (9%)
  matrix products  36.4 us (8%)
  between operations  17.5 us (4%)
  other arithmetic  17.4 us (4%)
    unnamed x5, waiting for transfers between devices  174 us
    all_gather x1, waiting for transfers between devices, body(): lax.all_gather(w_in, 'seq', axis=0, tiled=True)  82.3 us
    all_gather x2, waiting for transfers between devices, entering(): gathered = jax.tree.map(lambda a: lax.all_gather(a, axis), part)  48.7 us
    unnamed x60, local copies, waits for them, and re-layouts  25.9 us
    dynamic_slice x14, local copies, waits for them, and re-layouts, one(): lax.dynamic_index_in_dim(a, source, 0, False)  23 us
    psum x1, blocking collectives, body(): grad_rate, seq_squares = lax.psum((rate_part, squares), 'seq')  20 us
    unnamed x1, blocking collectives  19.4 us
  transfers between devices with their start and end apart: 4, of which 4 were waited for; matrix products, arithmetic and copies ran while one was open for 19% of the time, Pallas kernels for 0%

commit v1 on v0

v1 whole, which is shorter than its diff:
```python
import functools
import math

import jax
import jax.numpy as jnp
from jax import lax
from jax.experimental import pallas as pl
from jax.experimental.pallas import tpu as pltpu
from jax.sharding import PartitionSpec as P

P_SIZE = 64
LANES = 128
CHUNK = 256
MESH = pl.DeviceIdType.MESH
ascent = 0.05
rate_ascent = 0.5
F32 = jnp.float32
BF16 = jnp.bfloat16


def dot(a, b, ca=1, cb=0):
    return lax.dot_general(a, b, (((ca,), (cb,)), ((), ())), preferred_element_type=F32)


def split(a):
    high = a.astype(BF16)
    return high, (a - high.astype(F32)).astype(BF16)


def dot3(a, b, ca=1, cb=0):
    (ah, al), (bh, bl) = a, b
    return dot(ah, bh, ca, cb) + (dot(ah, bl, ca, cb) + dot(al, bh, ca, cb))


def loop(count, fn, start=0):
    def step(i, carry):
        fn(i)
        return carry

    lax.fori_loop(start, count, step, 0)


def mixer(
    n, nm, owners,
    tok, w, b, c, cot, lfull, dtfull, cumr, dtr,
    mixed, gw, rates,
    kern, scores, gx32, gxc, x_acc, x_bf, after, h_in,
    w_rx, tok_rx, gx_tx, gx_rx,
    dec_tx, dec_rx, lead_tx, lead_rx, after_tx, after_rx,
    st_tx, st_rx, h_tx, h_rx, pk_tx, pk_rx,
    w_s, w_r, tok_s, tok_r, gx_s, gx_r, dec_s, dec_r, lead_s, lead_r, af_s, af_r,
    st_s, st_r, h_s, h_r, pk_s, pk_r,
):
    me = lax.axis_index("seq")
    mm = lax.axis_index("mp")
    total = n * nm
    flat = me * nm + mm
    rows, width = cot.shape
    states = b.shape[1]
    pairs = width // LANES
    chunks = width // CHUNK
    piece = states // owners

    def copy(src, dst, ss, rs, peer):
        return pltpu.make_async_remote_copy(
            src_ref=src, dst_ref=dst, send_sem=ss, recv_sem=rs,
            device_id=(peer, mm), device_id_type=MESH,
        )

    def w_copy(peer, slot):
        return copy(w, w_rx.at[slot], w_s.at[peer], w_r.at[slot], peer)

    def tok_copy(peer, slot):
        return copy(tok.at[peer], tok_rx.at[slot], tok_s.at[peer], tok_r.at[slot], peer)

    def gx_copy(peer, slot):
        return copy(gx_tx, gx_rx.at[slot], gx_s.at[peer], gx_r.at[slot], peer)

    def dec_copy(peer, slot):
        return copy(dec_tx, dec_rx.at[slot], dec_s.at[peer], dec_r.at[slot], peer)

    def up_copy(tx, rx, ss, rs, peer, slot):
        return copy(tx.at[peer], rx.at[slot], ss.at[peer], rs.at[slot], peer)

    def pk_copy(peer_flat, slot):
        return pltpu.make_async_remote_copy(
            src_ref=pk_tx, dst_ref=pk_rx.at[slot], send_sem=pk_s.at[peer_flat],
            recv_sem=pk_r.at[slot], device_id=(peer_flat // nm, peer_flat % nm),
            device_id_type=MESH,
        )

    barrier = pltpu.get_barrier_semaphore()

    def greet(d):
        f = (flat + d) % total
        pl.semaphore_signal(barrier, inc=1, device_id=(f // nm, f % nm), device_id_type=MESH)

    loop(total, greet, 1)

    def chunk_ds(k):
        return pl.ds(pl.multiple_of(k * CHUNK, CHUNK), CHUNK)

    def pair_ds(k):
        return pl.ds(pl.multiple_of(k * LANES, LANES), LANES)

    def to_owner(tx, rx, ss, rs):
        def one(d):
            j = (me + d) % owners

            @pl.when(j != me)
            def _():
                up_copy(tx, rx, ss, rs, j, me).start()

            @pl.when(j == me)
            def _():
                rx[me] = tx[j]

        loop(owners, one)

    def owner_wait(tx, rx, ss, rs):
        def one(i):
            @pl.when(i != me)
            def _():
                up_copy(tx, rx, ss, rs, 0, i).wait_recv()

        loop(n, one)

    def from_owner(tx, rx, ss, rs):
        def one(d):
            j = (me + d) % n
            up_copy(tx, rx, ss, rs, j, me).start()

        rx[me] = tx[me]
        loop(n, one, 1)

    def from_owner_wait(tx, rx, ss, rs):
        def one(i):
            @pl.when(i != me)
            def _():
                up_copy(tx, rx, ss, rs, 0, i).wait_recv()

        loop(owners, one)

    def decay_row(j):
        d = dec_rx[j]
        return jnp.concatenate([d[k : k + 1, :] for k in range(pairs)], axis=1)

    final = lfull[rows - 1 : rows, :]
    dec = jnp.exp(final)
    for k in range(pairs):
        dec_tx[k : k + 1, :] = dec[:, k * LANES : (k + 1) * LANES]
    dec_rx[me] = dec_tx[...]
    b_val, c_val = b[...], c[...]
    b_split, c_split = split(b_val), split(c_val)
    bt_split, ct_split = split(b_val.T), split(c_val.T)

    def lead_chunk(k):
        ds = chunk_ds(k)
        lead = dot3(ct_split, split(cot[:, ds].astype(F32) * jnp.exp(lfull[:, ds])))
        for j in range(owners):
            lead_tx[j, :, ds] = lead[j * piece : (j + 1) * piece, :].astype(BF16)

    loop(chunks, lead_chunk)

    pl.semaphore_wait(barrier, total - 1)
    loop(n, lambda d: dec_copy((me + d) % n, me).start(), 1)
    to_owner(lead_tx, lead_rx, lead_s, lead_r)
    loop(n, lambda d: tok_copy((me + d) % n, me).start(), 1)

    scores[...] = dot3(c_split, b_split, 1, 1)
    lane = lax.broadcasted_iota(jnp.int32, (rows, LANES), 1)
    first = lane < P_SIZE

    def kern_pair(k):
        ds = pair_ds(k)
        level = lfull[:, ds]
        crow, drow = cumr[k], dtr[k]
        lower = lax.broadcasted_iota(jnp.int32, (rows, rows), 0) >= lax.broadcasted_iota(
            jnp.int32, (rows, rows), 1
        )
        cot_pair = cot[:, ds]
        parts = []
        for h in range(2):
            gap = level[:, h * P_SIZE : h * P_SIZE + 1] - crow[h : h + 1, :]
            blend = jnp.exp(jnp.where(lower, gap, -1e30))
            mat = (blend * (scores[...] * drow[h : h + 1, :])).astype(BF16)
            kern[2 * k + h] = mat
            parts.append(dot(mat, cot_pair, 0, 0))
        gx32[:, ds] = jnp.where(first, parts[0], parts[1])

    loop(pairs, kern_pair)

    loop(n, lambda d: dec_copy((me + d) % n, (me + n - d) % n).wait_recv(), 1)

    @pl.when(me < owners)
    def _():
        owner_wait(lead_tx, lead_rx, lead_s, lead_r)

        def step(i, acc):
            j = n - 1 - i
            after_tx[j] = acc.astype(BF16)
            return decay_row(j) * acc + lead_rx[j].astype(F32)

        lax.fori_loop(0, n, step, jnp.zeros((piece, width), F32))
        from_owner(after_tx, after_rx, af_s, af_r)

    loop(n, lambda d: w_copy((me + d) % n, me).start(), 1)
    from_owner_wait(after_tx, after_rx, af_s, af_r)
    for j in range(owners):
        after[j * piece : (j + 1) * piece, :] = after_rx[j]

    def gx_chunk(k):
        ds = chunk_ds(k)
        level = lfull[:, ds]
        a = after[:, ds]
        proj = dot(b_split[0], a) + dot(b_split[1], a)
        carry = dtfull[:, ds] * jnp.exp(level[rows - 1 : rows, :] - level) * proj
        gxc[:, ds] = carry
        whole = gx32[:, ds] + carry
        gx32[:, ds] = whole
        gx_tx[:, ds] = whole.astype(BF16)

    loop(chunks, gx_chunk)

    x_acc[...] = dot(tok[me], w[...], 0, 0)

    def project(d):
        src = (me + n - d) % n
        w_copy((me + d) % n, src).wait_recv()
        x_acc[...] += dot(tok[src], w_rx[src], 0, 0)

    loop(n, project, 1)

    def state_chunk(k):
        ds = chunk_ds(k)
        level = lfull[:, ds]
        x16 = x_acc[:, ds].astype(BF16)
        x_bf[:, ds] = x16
        tail = jnp.exp(level[rows - 1 : rows, :] - level) * dtfull[:, ds]
        state = dot3(bt_split, split(x16.astype(F32) * tail))
        for j in range(owners):
            st_tx[j, :, ds] = state[j * piece : (j + 1) * piece, :].astype(BF16)

    loop(chunks, state_chunk)
    to_owner(st_tx, st_rx, st_s, st_r)
    half = n // 2
    loop(half, lambda d: gx_copy((me + d) % n, me).start(), 1)

    def y_pair(k):
        ds = pair_ds(k)
        xp = x_bf[:, ds]
        x_acc[:, ds] = jnp.where(first, dot(kern[2 * k], xp), dot(kern[2 * k + 1], xp))

    loop(pairs, y_pair)

    @pl.when(me < owners)
    def _():
        owner_wait(st_tx, st_rx, st_s, st_r)

        def step(j, acc):
            h_tx[j] = acc.astype(BF16)
            return decay_row(j) * acc + st_rx[j].astype(F32)

        lax.fori_loop(0, n, step, jnp.zeros((piece, width), F32))
        from_owner(h_tx, h_rx, h_s, h_r)

    loop(n, lambda d: gx_copy((me + d) % n, me).start(), half)
    from_owner_wait(h_tx, h_rx, h_s, h_r)
    for j in range(owners):
        h_in[j * piece : (j + 1) * piece, :] = h_rx[j]

    pk_tx[...] = jnp.zeros(pk_tx.shape, F32)

    def out_chunk(k):
        ds = chunk_ds(k)
        level = lfull[:, ds]
        h = h_in[:, ds]
        y = x_acc[:, ds] + (dot(c_split[0], h) + dot(c_split[1], h)) * jnp.exp(level)
        mixed[:, ds] = y.astype(BF16)
        xs = x_bf[:, ds].astype(F32)
        last = level[rows - 1 : rows, :]
        inner = level * (y * cot[:, ds].astype(F32) - gx32[:, ds] * xs)
        part = jnp.sum(inner + last * (gxc[:, ds] * xs), axis=0, keepdims=True)
        cross = jnp.sum(after[:, ds].astype(F32) * h.astype(F32), axis=0, keepdims=True)
        part = part + jnp.exp(last) * last * cross
        for i in range(CHUNK // LANES):
            pk_tx[pl.ds(k * (CHUNK // LANES) + i, 1), :] = part[:, i * LANES : (i + 1) * LANES]

    loop(chunks, out_chunk)

    gw[...] = dot(tok[me], gx_tx[...])

    def weight(d):
        src = (me + n - d) % n
        tok_copy((me + d) % n, src).wait_recv()
        gx_copy((me + d) % n, src).wait_recv()
        gw[...] += dot(tok_rx[src], gx_rx[src])

    loop(n, weight, 1)
    square = jnp.zeros((1, LANES), F32)
    for k in range(pairs):
        g = gw[:, k * LANES : (k + 1) * LANES]
        square = square + jnp.sum(g * g, axis=0, keepdims=True)
    pk_tx[pairs : pairs + 1, :] = square
    pk_rx[flat] = pk_tx[...]
    loop(total, lambda d: pk_copy((flat + d) % total, flat).start(), 1)

    def sent(d):
        peer = (me + d) % n
        w_copy(peer, me).wait_send()
        tok_copy(peer, me).wait_send()
        gx_copy(peer, me).wait_send()
        dec_copy(peer, me).wait_send()

    loop(n, sent, 1)

    def sent_up(j):
        @pl.when(j != me)
        def _():
            up_copy(lead_tx, lead_rx, lead_s, lead_r, j, me).wait_send()
            up_copy(st_tx, st_rx, st_s, st_r, j, me).wait_send()

    loop(owners, sent_up)

    @pl.when(me < owners)
    def _():
        def sent_down(d):
            j = (me + d) % n
            up_copy(after_tx, after_rx, af_s, af_r, j, me).wait_send()
            up_copy(h_tx, h_rx, h_s, h_r, j, me).wait_send()

        loop(n, sent_down, 1)

    loop(total, lambda d: pk_copy((flat + d) % total, (flat + total - d) % total).wait_recv(), 1)
    for m in range(nm):
        acc = lax.fori_loop(
            0, n, lambda s, a: a + pk_rx[s * nm + m], jnp.zeros(pk_tx.shape, F32)
        )
        rates[m] = acc
    loop(total, lambda d: pk_copy((flat + d) % total, flat).wait_send(), 1)


def body(n, nm, tokens, w_in, b_in, c_in, dt, log_rate, cot):
    rows, model = tokens.shape
    depth, width = w_in.shape
    heads = dt.shape[0]
    states = b_in.shape[1]
    pairs = width // LANES
    owners = min(n, states // 16)
    piece = states // owners
    total = n * nm
    packet = (pairs + 8) // 8 * 8
    cum = jnp.cumsum(-dt * jnp.exp(log_rate)[:, None], axis=1)
    lfull = jnp.repeat(cum.T, P_SIZE, axis=1)
    dtfull = jnp.repeat(dt.T, P_SIZE, axis=1)
    tok = tokens.T.reshape(n, depth, rows)
    dma = pltpu.SemaphoreType.DMA
    vm = pltpu.VMEM
    scratch = [
        vm((heads, rows, rows), BF16),
        vm((rows, rows), F32),
        vm((rows, width), F32),
        vm((rows, width), F32),
        vm((rows, width), F32),
        vm((rows, width), BF16),
        vm((states, width), BF16),
        vm((states, width), BF16),
        vm((n, depth, width), BF16),
        vm((n, depth, rows), BF16),
        vm((rows, width), BF16),
        vm((n, rows, width), BF16),
        vm((pairs, LANES), F32),
        vm((n, pairs, LANES), F32),
        vm((owners, piece, width), BF16),
        vm((n, piece, width), BF16),
        vm((n, piece, width), BF16),
        vm((owners, piece, width), BF16),
        vm((owners, piece, width), BF16),
        vm((n, piece, width), BF16),
        vm((n, piece, width), BF16),
        vm((owners, piece, width), BF16),
        vm((packet, LANES), F32),
        vm((total, packet, LANES), F32),
    ] + [dma((n,))] * 16 + [dma((total,))] * 2
    spec = pl.BlockSpec(memory_space=pltpu.VMEM)
    mixed, grad_w, rates = pl.pallas_call(
        functools.partial(mixer, n, nm, owners),
        out_shape=(
            jax.ShapeDtypeStruct((rows, width), BF16),
            jax.ShapeDtypeStruct((depth, width), F32),
            jax.ShapeDtypeStruct((nm, packet, LANES), F32),
        ),
        in_specs=[spec] * 9,
        out_specs=(spec,) * 3,
        scratch_shapes=scratch,
        compiler_params=pltpu.CompilerParams(
            collective_id=0, has_side_effects=True, vmem_limit_bytes=67_000_000
        ),
    )(
        tok, w_in, b_in, c_in, cot, lfull, dtfull,
        cum.reshape(pairs, 2, rows), dt.reshape(pairs, 2, rows),
    )
    by_head = jnp.sum(rates[:, :pairs].reshape(nm, heads, P_SIZE), axis=2)
    rate_sq = jnp.sum(by_head * by_head)
    total_sq = jnp.sum(rates[:, pairs]) + rate_sq
    grad_rate = lax.dynamic_index_in_dim(by_head, lax.axis_index("mp"), 0, False)
    scale = 1.0 / jnp.maximum(jnp.sqrt(total_sq), 1.0)
    rate_scale = math.sqrt(heads * nm) / jnp.maximum(jnp.sqrt(rate_sq), 1.0)
    direction = grad_w * (math.sqrt(model * width * nm) * scale)
    perturbed = w_in.astype(F32) + ascent * scale * grad_w
    perturbed_rate = log_rate + rate_ascent * rate_scale * grad_rate
    return (mixed, direction, perturbed, perturbed_rate)


def solution(mesh):
    in_specs = (
        P("seq", None), P("seq", "mp"), P("seq", None), P("seq", None),
        P("mp", "seq"), P("mp"), P("seq", "mp"),
    )
    out_specs = (P("seq", "mp"), P("seq", "mp"), P("seq", "mp"), P("mp"))
    return jax.shard_map(
        functools.partial(body, mesh.shape["seq"], mesh.shape["mp"]),
        mesh=mesh, in_specs=in_specs, out_specs=out_specs, check_vma=False,
    )
```

time: 485 us -> 316 us (0.65)
  waiting for transfers between devices: 305 us -> 0 us
  Pallas kernels: 0 us -> 297 us
  local copies, waits for them, and re-layouts: 60 us -> 7.97 us
  blocking collectives: 45.7 us -> 0 us
  matrix products: 36.4 us -> 0 us
  between operations: 17.5 us -> 2.83 us
  other arithmetic: 17.4 us -> 7.55 us
    pallas_call x0 -> x1, Pallas kernels: none -> 297 us  [body(): pl.pallas_call(functools.partial(mixer, n, nm, owners), out_shape=(jax.Sh...]
    unnamed x5 -> x0, waiting for transfers between devices: 174 us -> none
    all_gather x3 -> x0, waiting for transfers between devices: 131 us -> none  [the longest x1 82.3 us: body(): lax.all_gather(w_in, 'seq', axis=0, tiled=True)]
    dot_general x10 -> x0, matrix products: 36.4 us -> none  [the longest x1 5.36 us: body(): lax.dot_general(columns, gx_bf, (((0,), (0,)), ((), ())), preferred_eleme...]
    psum x2 -> x0, blocking collectives: 26.3 us -> none  [the longest x1 20 us: body(): grad_rate, seq_squares = lax.psum((rate_part, squares), 'seq')]
    unnamed x60 -> x9, local copies, waits for them, and re-layouts: 25.9 us -> 0.86 us
    dynamic_slice x14 -> x0, local copies, waits for them, and re-layouts: 23 us -> none  [one(): lax.dynamic_index_in_dim(a, source, 0, False)]
    unnamed x1 -> x0, blocking collectives: 19.4 us -> none
  transfers between devices with their start and end apart: 4 -> 0, of which waited for: 4 -> 0; matrix products, arithmetic and copies ran while one was open for 19% -> 0% of each run, Pallas kernels for 0% -> 0%
where the time goes in v1:
time: 316 us; the launch traced here: 315 us
  Pallas kernels  297 us (94%)
  local copies, waits for them, and re-layouts  7.97 us (3%)
  other arithmetic  7.55 us (2%)
    pallas_call x1, Pallas kernels, body(): pl.pallas_call(functools.partial(mixer, n, nm, owners), out_shape=(jax.Sh...  297 us

profile of v1, /device:TPU:0, one launch (start us, length us, event | category | flops | bytes accessed | tf_op | source)
XLA Modules:
  0.0 315.3 jit_solution(1781158022530293687)
XLA Ops:
  0.6 0.7 exp.3
  1.3 0.8 copy_bitcast_fusion
  2.1 0.6 reduce-window.6
  2.7 0.2 slice_reduce_fusion
  2.9 0.1 bitcast_bitcast_fusion
  2.9 0.1 broadcast_in_dim.7
  3.0 0.0 copy-start.2
  3.0 1.3 copy.19.lfull
  4.3 0.1 broadcast_add_fusion
  4.4 0.6 reduce_window_sum.21.cumr
  5.1 0.0 copy-done.2
  5.1 0.1 broadcast_in_dim.8
  5.1 0.0 copy-start
  5.2 1.3 copy.20.dtfull
  6.5 0.0 copy-done
  6.5 1.4 copy.15
  8.0 0.6 reshape.46.dtr
  8.6 296.9 %shard_map.102 = (bf16[256,1024]{1,0:T(8,128)(2,1)}, f32[320,1024]{1,0:T(8,128)}, f32[4,16,128]{2,1,0:T(8,128)}) custom-call(bf16[8,320,256]{2,1,0:T(8,128)(2,1)} %bitcast.19, bf16[320,1024]{1,0:T(8,128)(2,1)} %w.1, f32[256,128]{1,0:T(8,128)} %b.1, f32[256,128]{1,0:T(8,128)} %c.1, bf16[256,1024]{1,0:T(8,128)(2,1)} %cot.1, f32[256,1024]{1,0:T(8,128)} %copy.19.lfull, ...), custom_call_target="tpu_custom_call" | custom-call | tf_op jit(solution)/shard_map/pallas_call | solution.py:386
  305.5 0.7 slice.15
  306.2 0.1 reshape.47
  306.3 0.1 reduce_sum.28
  306.4 0.6 multiply_reduce_fusion
  307.0 1.3 slice_reduce_fusion.1
  309.7 0.0 copy-start.3
  309.7 0.0 copy-start.1
  309.7 3.5 %multiply_add_fusion = (f32[320,1024]{1,0:T(8,128)}, f32[320,1024]{1,0:T(8,128)}) fusion(f32[320,1024]{1,0:T(8,128)} %get-tuple-element.8, bf16[320,1024]{1,0:T(8,128)(2,1)} %w.1, f32[]{:T(128)S(6)} %mul_shard_map.10, f32[]{:T(128)S(6)} %mul_shard_map.9), kind=kLoop, calls=%fused_computation | loop fusion | flops 1310720 | bytes 4587528 | tf_op jit(solution)/shard_map/add | solution.py:410
  313.9 0.0 copy-done.3
  313.9 0.5 bitcast_add_fusion
  314.5 0.0 copy-done.1
  314.5 0.8 copy.26
  (3 shorter events, 0.1 us)
Async XLA Ops:
  3.0 2.0 copy-start.2
  5.1 1.4 copy-start
  309.7 4.2 %copy-start.3 = (f32[16]{0:T(128)S(1)}, f32[16]{0:T(128)}, u32[]{:S(2)}) copy-start(f32[16]{0:T(128)} %param.12) | copy-start | bytes 196
  309.7 4.7 %copy-start.1 = (bf16[256,1024]{1,0:T(8,128)(2,1)S(1)}, bf16[256,1024]{1,0:T(8,128)(2,1)}, u32[]{:S(2)}) copy-start(bf16[256,1024]{1,0:T(8,128)(2,1)} %get-tuple-element.16) | copy-start | bytes 1572868
